TPU v7x, 32 devices: a whole 2x2x4 slice. The times are simulated.
32 devices in a mesh: seq: 8 (over z, core), ch: 4 (over y, x).
Axes of the slice: x: 2, y: 2, z: 4, core: 2. Of those that a mesh axis runs over, the one named last changes fastest.
Arguments:
- input_q: bfloat16 [4096, 8192], P('seq', 'ch'), may hold values from -6 to 6
- input_k: bfloat16 [4096, 8192], P('seq', 'ch'), may hold values from -6 to 6
- input_v: bfloat16 [4096, 8192], P('seq', 'ch'), may hold values from -6 to 6
- grad_out: bfloat16 [4096, 8192], P('seq', 'ch'), may hold values from -6 to 6
- short_filters: float32 [3, 3, 8192], P(None, None, 'ch'), may hold values from -3.5 to 3.5
- long_filter: float32 [128, 8192], P(None, 'ch'), may hold values from -0.5 to 0.5
- skip_gain: float32 [8192], P('ch'), may hold values from 0.5 to 1.5
Outputs:
- grad_input_q: bfloat16 [4096, 8192], P('seq', 'ch')
- grad_input_k: bfloat16 [4096, 8192], P('seq', 'ch')
- grad_input_v: bfloat16 [4096, 8192], P('seq', 'ch')
- grad_long: float32 [128, 8192], P('seq', 'ch')
- grad_short: float32 [3, 3, 8192], P(None, None, 'ch')
- grad_skip: float32 [8192], P('ch')
All inputs are finite; a program needn't handle non-finite values.
Results may differ from a plain program's by a relative error of at most 0.001.
Values may be sent and summed in bfloat16 or wider, within the bound.
No kernel may reach another device: no remote copies, remote signals or barrier semaphores. Data moves between devices by JAX's collectives and lax.ppermute only.
A program may use at most 128 MiB of HBM per device.

v0:
```python
import functools

import jax
import jax.numpy as jnp
import numpy as np
from jax import lax
from jax.experimental import pallas as pl
from jax.experimental.pallas import tpu as pltpu
from jax.sharding import PartitionSpec as P

CHUNKS = 2
LANES = 256
EDGE = 16
F32 = jnp.float32
BF16 = jnp.bfloat16


def split_np(m):
    hi = np.asarray(m, np.float32).astype(BF16)
    lo = (np.asarray(m, np.float64) - hi.astype(np.float64)).astype(np.float32).astype(BF16)
    return hi, lo


def matrices(n):
    w = 2.0 * np.pi * (np.arange(n) + 0.25) / n
    ang = np.outer(w, np.arange(n))
    fwd = np.concatenate([np.cos(ang), -np.sin(ang)], 0)
    inv = np.concatenate([np.cos(ang).T, -np.sin(ang).T], 1) / n
    fh, fl = split_np(fwd)
    ih, il = split_np(inv)
    return np.concatenate([fh, fh, fl], 1), np.concatenate([ih, ih, il], 1)


def dot3(mat, x):
    hi = x.astype(BF16)
    lo = (x - hi.astype(F32)).astype(BF16)
    return jnp.dot(mat, jnp.concatenate([hi, lo, hi], 0), preferred_element_type=F32)


def kernel(span, length, nalias, q_r, k_r, v_r, g_r, fwd_r, bwd_r, sf_r, h_r, hrev_r, fm_r, im_r, *rest):
    rest = rest[nalias:]
    oq_r, ok_r, ov_r, pl_r, ps_r = rest[:5]
    xq, xk, xv, kf, vf, zs, gs, gq, gk, gv, zsp, gsp = rest[5:]
    n = span
    nb = length // n
    halo = n + EDGE
    xq[0:EDGE] = fwd_r[2 * halo :].astype(F32)
    xq[EDGE : EDGE + length] = q_r[...].astype(F32)
    xq[EDGE + length :] = bwd_r[0:halo].astype(F32)
    xk[0:halo] = fwd_r[0:halo].astype(F32)
    xk[halo : halo + length] = k_r[...].astype(F32)
    xk[halo + length :] = bwd_r[2 * halo : 2 * halo + EDGE].astype(F32)
    xv[0:halo] = fwd_r[halo : 2 * halo].astype(F32)
    xv[halo : halo + length] = v_r[...].astype(F32)
    xv[halo + length :] = bwd_r[2 * halo + EDGE :].astype(F32)
    taps = sf_r.shape[1]
    sf = [[sf_r[a, i : i + 1, :] for i in range(taps)] for a in range(3)]
    fm = fm_r[...]
    im = im_r[...]

    def feat(ref, base, t0, rows, w):
        acc = w[0] * ref[base + t0 : base + t0 + rows]
        for i in range(1, taps):
            acc = acc + w[i] * ref[base + t0 - i : base + t0 - i + rows]
        return acc

    for b in range(-1, nb):
        t0 = b * n
        kb = feat(xk, halo, t0, n, sf[1])
        vb = feat(xv, halo, t0, n, sf[2])
        zb = kb * vb
        if b >= 0:
            kf[t0 : t0 + n] = kb
            vf[t0 : t0 + n] = vb
        zs[t0 + n : t0 + 2 * n] = zb
        zsp[b + 1] = dot3(fm, zb)
    kb = feat(xk, halo, length, 8, sf[1])
    vb = feat(xv, halo, length, 8, sf[2])
    kf[length : length + 8] = kb
    vf[length : length + 8] = vb
    zs[length + n : length + n + 8] = kb * vb
    for b in range(nb + 1):
        t0 = b * n
        qb = feat(xq, EDGE, t0, n, sf[0])
        gb = g_r[t0 : t0 + n] if b < nb else bwd_r[halo : halo + n]
        gsb = qb * gb.astype(F32)
        gs[t0 : t0 + n] = gsb
        gsp[b] = dot3(fm, gsb)
    t0 = length + n
    qb = feat(xq, EDGE, t0, 8, sf[0])
    gs[t0 : t0 + 8] = qb * bwd_r[halo + n : halo + n + EDGE].astype(F32)[0:8]

    h = h_r[...]
    hsp = dot3(fm, h)
    hr, hi = hsp[0:n], hsp[n:]
    lr = li = None
    for b in range(nb):
        t0 = b * n
        zc, zp = zsp.at[b + 1], zsp.at[b]
        gc, gn = gsp.at[b], gsp.at[b + 1]
        ur = zc[0:n] - zp[n:]
        ui = zc[n:] + zp[0:n]
        gr, gi = gc[0:n], gc[n:]
        dr = gr * ur + gi * ui
        di = gi * ur - gr * ui
        lr = dr if lr is None else lr + dr
        li = di if li is None else li + di
        s = dot3(im, jnp.concatenate([hr * ur - hi * ui, hr * ui + hi * ur], 0))
        gq[t0 : t0 + n] = s * g_r[t0 : t0 + n].astype(F32)
        wr = gr + gn[n:]
        wi = gi - gn[0:n]
        gz = dot3(im, jnp.concatenate([hr * wr + hi * wi, hr * wi - hi * wr], 0))
        gk[t0 : t0 + n] = gz * vf[t0 : t0 + n]
        gv[t0 : t0 + n] = gz * kf[t0 : t0 + n]
    long = dot3(im, jnp.concatenate([lr, li], 0))
    pl_r[...] = long

    hrev = hrev_r[...]
    g_edge = bwd_r[halo : halo + EDGE].astype(F32)
    for r in range(taps - 1):
        at = length + n - (n - 1) + r
        sr = jnp.sum(hrev * zs[at : at + n], 0, keepdims=True)
        gzr = jnp.sum(h * gs[length + r : length + r + n], 0, keepdims=True)
        gq[length + r : length + r + 1] = sr * g_edge[r : r + 1]
        gk[length + r : length + r + 1] = gzr * vf[length + r : length + r + 1]
        gv[length + r : length + r + 1] = gzr * kf[length + r : length + r + 1]

    rows = []
    for a, (grad, x, base, out) in enumerate(((gq, xq, EDGE, oq_r), (gk, xk, halo, ok_r), (gv, xv, halo, ov_r))):
        sums = [None] * taps
        for b in range(nb):
            t0 = b * n
            own = grad[t0 : t0 + n]
            acc = sf[a][0] * own
            for i in range(1, taps):
                acc = acc + sf[a][i] * grad[t0 + i : t0 + i + n]
            out[t0 : t0 + n] = acc.astype(BF16)
            for i in range(taps):
                part = jnp.sum(own * x[base + t0 - i : base + t0 - i + n], 0, keepdims=True)
                sums[i] = part if sums[i] is None else sums[i] + part
        rows += sums
    rows.append(long[0:1])
    for i, row in enumerate(rows):
        ps_r[i : i + 1] = row


def shifted(value, axis, by):
    size = lax.axis_size(axis)
    pairs = [(i, i + by) for i in range(size) if 0 <= i + by < size]
    return lax.ppermute(value, axis, pairs)


def reduce_parts(long, small, axis):
    size = lax.axis_size(axis)
    me = lax.axis_index(axis)
    if size & (size - 1):
        return lax.psum_scatter(long, axis, scatter_dimension=0, tiled=True), lax.psum(small, axis)
    piece = long.shape[0] // size
    width = long.shape[1]
    cur = long.reshape((size, piece, width))
    dist = 1
    while dist < size:
        bit = (me // dist) % 2
        pair = cur.reshape((cur.shape[0] // 2, 2, piece, width))
        keep = jnp.where(bit == 0, pair[:, 0], pair[:, 1])
        send = jnp.where(bit == 0, pair[:, 1], pair[:, 0])
        half = keep.shape[0]
        pack = jnp.concatenate([send.reshape(half * piece, width), small], 0)
        got = lax.ppermute(pack, axis, [(i, i ^ dist) for i in range(size)])
        cur = keep + got[: half * piece].reshape(half, piece, width)
        small = small + got[half * piece :]
        dist *= 2
    return cur[0], small


def body(input_q, input_k, input_v, grad_out, short_filters, long_filter, skip_gain):
    length, width = input_q.shape
    taps = short_filters.shape[1]
    n = long_filter.shape[0]
    halo = n + EDGE
    lanes = LANES
    cw = width // CHUNKS
    steps = cw // lanes
    fm, im = matrices(n)
    fm = jnp.asarray(fm)
    im = jnp.asarray(im)
    hg = long_filter.at[0].add(skip_gain)
    hrev = hg[::-1]
    arrays = (input_q, input_k, input_v, grad_out)
    outs = ()
    halos = []
    for c in range(CHUNKS):
        cs = slice(c * cw, (c + 1) * cw)
        tail = jnp.concatenate([input_k[length - halo :, cs], input_v[length - halo :, cs], input_q[length - EDGE :, cs]], 0)
        head = jnp.concatenate([input_q[:halo, cs], grad_out[:halo, cs], input_k[:EDGE, cs], input_v[:EDGE, cs]], 0)
        halos.append((shifted(tail, "seq", 1), shifted(head, "seq", -1)))
    small_rows = 3 * taps + 1
    parts = []
    for c in range(CHUNKS):
        col = lambda i, c=c: (0, c * steps + i)
        own = lambda i: (0, i)
        full = pl.BlockSpec((length, lanes), col)
        fixed = lambda a: pl.BlockSpec(a.shape, lambda i: (0, 0))
        fwd, bwd = halos[c]
        res = pl.pallas_call(
            functools.partial(kernel, n, length, len(outs)),
            grid=(steps,),
            in_specs=[full] * 4
            + [
                pl.BlockSpec((fwd.shape[0], lanes), own),
                pl.BlockSpec((bwd.shape[0], lanes), own),
                pl.BlockSpec((3, taps, lanes), lambda i, c=c: (0, 0, c * steps + i)),
                pl.BlockSpec((n, lanes), col),
                pl.BlockSpec((n, lanes), col),
                fixed(fm),
                fixed(im),
            ]
            + [pl.BlockSpec(memory_space=pl.ANY)] * len(outs),
            out_specs=[full] * 3 + [pl.BlockSpec((n, lanes), own), pl.BlockSpec((small_rows, lanes), own)],
            out_shape=[jax.ShapeDtypeStruct((length, width), BF16)] * 3
            + [jax.ShapeDtypeStruct((n, cw), F32), jax.ShapeDtypeStruct((small_rows, cw), F32)],
            scratch_shapes=[
                pltpu.VMEM((EDGE + length + halo, lanes), F32),
                pltpu.VMEM((halo + length + EDGE, lanes), F32),
                pltpu.VMEM((halo + length + EDGE, lanes), F32),
                pltpu.VMEM((length + 8, lanes), F32),
                pltpu.VMEM((length + 8, lanes), F32),
                pltpu.VMEM((n + length + 8, lanes), F32),
                pltpu.VMEM((length + n + 8, lanes), F32),
                pltpu.VMEM((length + 8, lanes), F32),
                pltpu.VMEM((length + 8, lanes), F32),
                pltpu.VMEM((length + 8, lanes), F32),
                pltpu.VMEM((length // n + 1, 2 * n, lanes), F32),
                pltpu.VMEM((length // n + 1, 2 * n, lanes), F32),
            ],
            input_output_aliases={11 + j: j for j in range(len(outs))},
            name=f"hyena_bwd_{c}",
        )(*arrays, fwd, bwd, short_filters, hg, hrev, fm, im, *outs)
        outs = tuple(res[:3])
        parts.append(reduce_parts(res[3], res[4], "seq"))
    grad_long = jnp.concatenate([p[0] for p in parts], 1)
    small = jnp.concatenate([p[1] for p in parts], 1)
    return outs + (grad_long, small[: 3 * taps].reshape(3, taps, width), small[3 * taps])


def solution(mesh):
    return jax.shard_map(
        body,
        mesh=mesh,
        in_specs=(
            P("seq", "ch"),
            P("seq", "ch"),
            P("seq", "ch"),
            P("seq", "ch"),
            P(None, None, "ch"),
            P(None, "ch"),
            P("ch"),
        ),
        out_specs=(
            P("seq", "ch"),
            P("seq", "ch"),
            P("seq", "ch"),
            P("seq", "ch"),
            P(None, None, "ch"),
            P("ch"),
        ),
        check_vma=False,
    )
```

profile of v0, /device:TPU:0, one launch (start us, length us, event | category | flops | bytes accessed | tf_op | source)
XLA Modules:
  0.0 91.5 jit_solution(8759077980135828454)
XLA Ops:
  0.6 1.2 %copy.44 = f32[128,2048]{1,0:T(8,128)S(1)} copy(f32[128,2048]{1,0:T(8,128)} %param.16) | data formatting | bytes 2097152
  1.9 1.1 %fusion.4 = (bf16[144,1024]{1,0:T(8,128)(2,1)S(1)}, bf16[144,1024]{1,0:T(8,128)(2,1)S(1)}) fusion(bf16[512,2048]{1,0:T(8,128)(2,1)} %q_r.3), kind=kLoop, calls=%fused_computation.38 | loop fusion | bytes 1179648 | tf_op jit(solution)/shard_map/slice | solution.py:195
  3.0 1.1 %fusion.5 = (bf16[144,1024]{1,0:T(8,128)(2,1)S(1)}, bf16[144,1024]{1,0:T(8,128)(2,1)S(1)}) fusion(bf16[512,2048]{1,0:T(8,128)(2,1)} %g_r.3), kind=kLoop, calls=%fused_computation.39 | loop fusion | bytes 1179648 | tf_op jit(solution)/shard_map/slice | solution.py:195
  4.0 0.8 fusion.6
  4.9 1.3 %collective-permute-start.3 = (bf16[320,1024]{1,0:T(8,128)(2,1)S(1)}, bf16[320,1024]{1,0:T(8,128)(2,1)S(1)}, u32[]{:S(2)}, u32[]{:S(2)}) collective-permute-start(bf16[320,1024]{1,0:T(8,128)(2,1)S(1)} %pad_maximum_fusion.1), channel_id=1, source_target_pairs={{4,0},{8,4},{12,8},{16,12},{20,16},{24,20},{28,24},{5,1},{9,5},{13... | collective-permute-start | bytes 1966088 | tf_op jit(solution)/shard_map/ppermute | solution.py:150
  6.2 1.3 %fusion.8 = (bf16[144,1024]{1,0:T(8,128)(2,1)S(1)}, bf16[144,1024]{1,0:T(8,128)(2,1)S(1)}, bf16[144,1024]{1,0:T(8,128)(2,1)S(1)}, bf16[144,1024]{1,0:T(8,128)(2,1)S(1)}) fusion(bf16[512,2048]{1,0:T(8,128)(2,1)} %k_r.3, bf16[512,2048]{1,0:T(8,128)(2,1)} %v_r.3), kind=kLoop, calls=%fused_computation.42 | loop fusion | bytes 2359296 | tf_op jit(solution)/shard_map/slice | solution.py:194
  7.6 0.8 fusion.10
  8.4 0.9 pad_maximum_fusion.3
  9.2 3.9 %collective-permute-start.2 = (bf16[304,1024]{1,0:T(8,128)(2,1)}, bf16[304,1024]{1,0:T(8,128)(2,1)}, u32[]{:S(2)}, u32[]{:S(2)}) collective-permute-start(bf16[304,1024]{1,0:T(8,128)(2,1)} %pad_maximum_fusion.3), channel_id=1, source_target_pairs={{0,4},{4,8},{8,12},{12,16},{16,20},{20,24},{24,28},{1,5},{5,9},{9,... | collective-permute-start | bytes 1867784 | tf_op jit(solution)/shard_map/ppermute | solution.py:150
  13.1 0.0 copy-start.5
  13.1 0.9 pad_maximum_fusion
  14.0 1.3 %collective-permute-start.1 = (bf16[320,1024]{1,0:T(8,128)(2,1)}, bf16[320,1024]{1,0:T(8,128)(2,1)S(1)}, u32[]{:S(2)}, u32[]{:S(2)}) collective-permute-start(bf16[320,1024]{1,0:T(8,128)(2,1)} %pad_maximum_fusion), channel_id=1, source_target_pairs={{4,0},{8,4},{12,8},{16,12},{20,16},{24,20},{28,24},{5,1},{9,5},{13... | collective-permute-start | bytes 1966088 | tf_op jit(solution)/shard_map/ppermute | solution.py:150
  15.3 0.9 pad_maximum_fusion.2
  16.2 5.2 %collective-permute-start = (bf16[304,1024]{1,0:T(8,128)(2,1)}, bf16[304,1024]{1,0:T(8,128)(2,1)}, u32[]{:S(2)}, u32[]{:S(2)}) collective-permute-start(bf16[304,1024]{1,0:T(8,128)(2,1)} %pad_maximum_fusion.2), channel_id=1, source_target_pairs={{0,4},{4,8},{8,12},{12,16},{16,20},{20,24},{24,28},{1,5},{5,9},{9,... | collective-permute-start | bytes 1867784 | tf_op jit(solution)/shard_map/ppermute | solution.py:150
  21.4 0.0 copy-done.5
  21.4 0.2 scatter-add.4.h_r
  21.6 0.0 copy-start
  21.6 5.4 %rev.3.hrev_r = f32[128,2048]{1,0:T(8,128)} reverse(f32[128,2048]{1,0:T(8,128)S(1)} %scatter-add.4.h_r), dimensions={0} | reverse | bytes 2097152 | tf_op jit(solution)/shard_map/rev | solution.py:188
  27.0 0.0 collective-permute-done.2.fwd_r
  27.0 0.0 collective-permute-done.3.bwd_r
  27.0 0.0 copy-done
  27.0 0.0 copy-start.2
  27.0 0.8 copy-done.2
  27.8 16.6 %hyena_bwd_0.1 = (bf16[512,2048]{1,0:T(8,128)(2,1)}, bf16[512,2048]{1,0:T(8,128)(2,1)}, bf16[512,2048]{1,0:T(8,128)(2,1)}, f32[128,1024]{1,0:T(8,128)}, f32[10,1024]{1,0:T(8,128)}) custom-call(bf16[512,2048]{1,0:T(8,128)(2,1)} %q_r.3, bf16[512,2048]{1,0:T(8,128)(2,1)} %k_r.3, bf16[512,2048]{1,0:T(8,128)(2,1)} %v_r.3, bf16[512,2048]{1,0:T(8,128)(2,1)} %g_r.3, ...), custom_call_target="tpu_custom_call" | custom-call | tf_op jit(solution)/shard_map/hyena_bwd_0/pallas_call | solution.py:205
  44.4 1.1 %fusion.1 = (f32[4,1,16,1024]{3,2,0,1:T(8,128)S(1)}, f32[4,1,16,1024]{3,2,0,1:T(8,128)S(1)}) fusion(f32[4,2,16,1024]{3,2,1,0:T(8,128)} %bitcast.61, pred[]{:T(512)S(6)} %eq.27), kind=kLoop, calls=%fused_computation.13 | loop fusion | flops 131072 | bytes 1048577 | tf_op jit(solution)/shard_map/jit(_where)/select_n | solution.py:165
  45.5 0.9 pad_maximum_fusion.4
  46.3 1.0 %collective-permute-start.4 = (f32[74,1024]{1,0:T(8,128)S(1)}, f32[74,1024]{1,0:T(8,128)S(1)}, u32[]{:S(2)}, u32[]{:S(2)}) collective-permute-start(f32[74,1024]{1,0:T(8,128)S(1)} %pad_maximum_fusion.4), channel_id=1, source_target_pairs={{0,4},{4,0},{8,12},{12,8},{16,20},{20,16},{24,28},{28,24},{1,5},{5... | collective-permute-start | bytes 909320 | tf_op jit(solution)/shard_map/ppermute | solution.py:169
  47.4 0.0 collective-permute-done.fwd_r
  47.4 0.0 collective-permute-done.1.bwd_r
  47.4 0.0 copy-start.1
  47.4 0.9 copy-done.1
  48.2 16.6 %hyena_bwd_1.1 = (bf16[512,2048]{1,0:T(8,128)(2,1)}, bf16[512,2048]{1,0:T(8,128)(2,1)}, bf16[512,2048]{1,0:T(8,128)(2,1)}, f32[128,1024]{1,0:T(8,128)}, f32[10,1024]{1,0:T(8,128)}) custom-call(bf16[512,2048]{1,0:T(8,128)(2,1)} %q_r.3, bf16[512,2048]{1,0:T(8,128)(2,1)} %k_r.3, ...), custom_call_target="tpu_custom_call", output_to_operand_aliasing={{0}: (11, {}), {1}: (12, {}), {2}: (13, {})} | custom-call | tf_op jit(solution)/shard_map/hyena_bwd_1/pallas_call | solution.py:205
  64.9 1.1 %fusion.3 = (f32[4,1,16,1024]{3,2,0,1:T(8,128)S(1)}, f32[4,1,16,1024]{3,2,0,1:T(8,128)S(1)}) fusion(f32[4,2,16,1024]{3,2,1,0:T(8,128)} %bitcast.60, pred[]{:T(512)S(6)} %eq.27), kind=kLoop, calls=%fused_computation.15 | loop fusion | flops 131072 | bytes 1048577 | tf_op jit(solution)/shard_map/jit(_where)/select_n | solution.py:165
  66.0 0.0 copy-start.3
  66.0 0.9 pad_maximum_fusion.5
  66.9 0.1 collective-permute-start.7
  67.0 0.0 collective-permute-done.4
  67.0 0.0 copy-start.4
  67.1 0.0 copy-done.3
  67.1 1.6 %collective-permute-start.5 = (f32[42,1024]{1,0:T(8,128)S(1)}, f32[42,1024]{1,0:T(8,128)S(1)}, u32[]{:S(2)}, u32[]{:S(2)}) collective-permute-start(f32[42,1024]{1,0:T(8,128)S(1)} %pad_maximum_fusion.6), channel_id=1, source_target_pairs={{0,8},{4,12},{8,0},{12,4},{16,24},{20,28},{24,16},{28,20},{1,9},{5... | collective-permute-start | bytes 516104 | tf_op jit(solution)/shard_map/ppermute | solution.py:169
  68.8 0.0 collective-permute-done.7
  68.9 0.0 copy-done.4
  68.9 1.4 %collective-permute-start.8 = (f32[42,1024]{1,0:T(8,128)S(1)}, f32[42,1024]{1,0:T(8,128)S(1)}, u32[]{:S(2)}, u32[]{:S(2)}) collective-permute-start(f32[42,1024]{1,0:T(8,128)S(1)} %pad_maximum_fusion.7), channel_id=1, source_target_pairs={{0,8},{4,12},{8,0},{12,4},{16,24},{20,28},{24,16},{28,20},{1,9},{5... | collective-permute-start | bytes 516104 | tf_op jit(solution)/shard_map/ppermute | solution.py:169
  70.4 4.6 %collective-permute-done.5 = f32[42,1024]{1,0:T(8,128)S(1)} collective-permute-done((f32[42,1024]{1,0:T(8,128)S(1)}, f32[42,1024]{1,0:T(8,128)S(1)}, u32[]{:S(2)}, u32[]{:S(2)}) %collective-permute-start.5) | collective-permute-done | bytes 172064 | tf_op jit(solution)/shard_map/ppermute | solution.py:169
  75.1 2.7 %collective-permute-start.6 = (f32[26,1024]{1,0:T(8,128)S(1)}, f32[26,1024]{1,0:T(8,128)S(1)}, u32[]{:S(2)}, u32[]{:S(2)}) collective-permute-start(f32[26,1024]{1,0:T(8,128)S(1)} %pad_maximum_fusion.8), channel_id=1, source_target_pairs={{0,16},{4,20},{8,24},{12,28},{16,0},{20,4},{24,8},{28,12},{1,17},{... | collective-permute-start | bytes 319496 | tf_op jit(solution)/shard_map/ppermute | solution.py:169
  77.7 3.6 %collective-permute-done.8 = f32[42,1024]{1,0:T(8,128)S(1)} collective-permute-done((f32[42,1024]{1,0:T(8,128)S(1)}, f32[42,1024]{1,0:T(8,128)S(1)}, u32[]{:S(2)}, u32[]{:S(2)}) %collective-permute-start.8) | collective-permute-done | bytes 172064 | tf_op jit(solution)/shard_map/ppermute | solution.py:169
  81.4 0.5 collective-permute-start.9
  81.9 4.9 %collective-permute-done.6 = f32[26,1024]{1,0:T(8,128)S(1)} collective-permute-done((f32[26,1024]{1,0:T(8,128)S(1)}, f32[26,1024]{1,0:T(8,128)S(1)}, u32[]{:S(2)}, u32[]{:S(2)}) %collective-permute-start.6) | collective-permute-done | bytes 106528 | tf_op jit(solution)/shard_map/ppermute | solution.py:169
  86.8 2.6 %collective-permute-done.9 = f32[26,1024]{1,0:T(8,128)S(1)} collective-permute-done((f32[26,1024]{1,0:T(8,128)S(1)}, f32[26,1024]{1,0:T(8,128)S(1)}, u32[]{:S(2)}, u32[]{:S(2)}) %collective-permute-start.9) | collective-permute-done | bytes 106528 | tf_op jit(solution)/shard_map/ppermute | solution.py:169
  89.4 0.6 pad_maximum_fusion.11
  90.1 0.7 reshape.187
  90.8 0.7 pad_maximum_fusion.10
  (27 shorter events, 0.4 us)
Async XLA Ops:
  4.9 22.0 %collective-permute-start.3 = (bf16[320,1024]{1,0:T(8,128)(2,1)S(1)}, bf16[320,1024]{1,0:T(8,128)(2,1)S(1)}, u32[]{:S(2)}, u32[]{:S(2)}) collective-permute-start(bf16[320,1024]{1,0:T(8,128)(2,1)S(1)} %pad_maximum_fusion.1), channel_id=1, source_target_pairs={{4,0},{8,4},{12,8},{16,12},{20,16},{24,20},{28,24},{5,1},{9,5},{13... | collective-permute-start | bytes 1966088 | tf_op jit(solution)/shard_map/ppermute | solution.py:150
  9.2 17.7 %collective-permute-start.2 = (bf16[304,1024]{1,0:T(8,128)(2,1)}, bf16[304,1024]{1,0:T(8,128)(2,1)}, u32[]{:S(2)}, u32[]{:S(2)}) collective-permute-start(bf16[304,1024]{1,0:T(8,128)(2,1)} %pad_maximum_fusion.3), channel_id=1, source_target_pairs={{0,4},{4,8},{8,12},{12,16},{16,20},{20,24},{24,28},{1,5},{5,9},{9,... | collective-permute-start | bytes 1867784 | tf_op jit(solution)/shard_map/ppermute | solution.py:150
  13.1 8.3 %copy-start.5 = (f32[2048]{0:T(1024)S(1)}, f32[2048]{0:T(1024)}, u32[]{:S(2)}) copy-start(f32[2048]{0:T(1024)} %param.17) | copy-start | bytes 24580
  14.0 33.4 %collective-permute-start.1 = (bf16[320,1024]{1,0:T(8,128)(2,1)}, bf16[320,1024]{1,0:T(8,128)(2,1)S(1)}, u32[]{:S(2)}, u32[]{:S(2)}) collective-permute-start(bf16[320,1024]{1,0:T(8,128)(2,1)} %pad_maximum_fusion), channel_id=1, source_target_pairs={{4,0},{8,4},{12,8},{16,12},{20,16},{24,20},{28,24},{5,1},{9,5},{13... | collective-permute-start | bytes 1966088 | tf_op jit(solution)/shard_map/ppermute | solution.py:150
  16.2 31.2 %collective-permute-start = (bf16[304,1024]{1,0:T(8,128)(2,1)}, bf16[304,1024]{1,0:T(8,128)(2,1)}, u32[]{:S(2)}, u32[]{:S(2)}) collective-permute-start(bf16[304,1024]{1,0:T(8,128)(2,1)} %pad_maximum_fusion.2), channel_id=1, source_target_pairs={{0,4},{4,8},{8,12},{12,16},{16,20},{20,24},{24,28},{1,5},{5,9},{9,... | collective-permute-start | bytes 1867784 | tf_op jit(solution)/shard_map/ppermute | solution.py:150
  21.6 5.4 %copy-start = (f32[128,2048]{1,0:T(8,128)}, f32[128,2048]{1,0:T(8,128)S(1)}, u32[]{:S(2)}) copy-start(f32[128,2048]{1,0:T(8,128)S(1)} %scatter-add.4.h_r) | copy-start | bytes 3145732
  27.0 0.8 copy-start.2
  46.3 20.6 %collective-permute-start.4 = (f32[74,1024]{1,0:T(8,128)S(1)}, f32[74,1024]{1,0:T(8,128)S(1)}, u32[]{:S(2)}, u32[]{:S(2)}) collective-permute-start(f32[74,1024]{1,0:T(8,128)S(1)} %pad_maximum_fusion.4), channel_id=1, source_target_pairs={{0,4},{4,0},{8,12},{12,8},{16,20},{20,16},{24,28},{28,24},{1,5},{5... | collective-permute-start | bytes 909320 | tf_op jit(solution)/shard_map/ppermute | solution.py:169
  47.4 0.9 copy-start.1
  66.0 1.1 %copy-start.3 = (f32[10,1024]{1,0:T(8,128)S(1)}, f32[10,1024]{1,0:T(8,128)}, u32[]{:S(2)}) copy-start(f32[10,1024]{1,0:T(8,128)} %get-tuple-element.35) | copy-start | bytes 122884
  66.9 1.9 %collective-permute-start.7 = (f32[74,1024]{1,0:T(8,128)S(1)}, f32[74,1024]{1,0:T(8,128)S(1)}, u32[]{:S(2)}, u32[]{:S(2)}) collective-permute-start(f32[74,1024]{1,0:T(8,128)S(1)} %pad_maximum_fusion.5), channel_id=1, source_target_pairs={{0,4},{4,0},{8,12},{12,8},{16,20},{20,16},{24,28},{28,24},{1,5},{5... | collective-permute-start | bytes 909320 | tf_op jit(solution)/shard_map/ppermute | solution.py:169
  67.0 1.8 %copy-start.4 = (f32[10,1024]{1,0:T(8,128)S(1)}, f32[10,1024]{1,0:T(8,128)}, u32[]{:S(2)}) copy-start(f32[10,1024]{1,0:T(8,128)} %get-tuple-element.37) | copy-start | bytes 122884
  67.1 7.8 %collective-permute-start.5 = (f32[42,1024]{1,0:T(8,128)S(1)}, f32[42,1024]{1,0:T(8,128)S(1)}, u32[]{:S(2)}, u32[]{:S(2)}) collective-permute-start(f32[42,1024]{1,0:T(8,128)S(1)} %pad_maximum_fusion.6), channel_id=1, source_target_pairs={{0,8},{4,12},{8,0},{12,4},{16,24},{20,28},{24,16},{28,20},{1,9},{5... | collective-permute-start | bytes 516104 | tf_op jit(solution)/shard_map/ppermute | solution.py:169
  68.9 12.4 %collective-permute-start.8 = (f32[42,1024]{1,0:T(8,128)S(1)}, f32[42,1024]{1,0:T(8,128)S(1)}, u32[]{:S(2)}, u32[]{:S(2)}) collective-permute-start(f32[42,1024]{1,0:T(8,128)S(1)} %pad_maximum_fusion.7), channel_id=1, source_target_pairs={{0,8},{4,12},{8,0},{12,4},{16,24},{20,28},{24,16},{28,20},{1,9},{5... | collective-permute-start | bytes 516104 | tf_op jit(solution)/shard_map/ppermute | solution.py:169
  75.1 11.7 %collective-permute-start.6 = (f32[26,1024]{1,0:T(8,128)S(1)}, f32[26,1024]{1,0:T(8,128)S(1)}, u32[]{:S(2)}, u32[]{:S(2)}) collective-permute-start(f32[26,1024]{1,0:T(8,128)S(1)} %pad_maximum_fusion.8), channel_id=1, source_target_pairs={{0,16},{4,20},{8,24},{12,28},{16,0},{20,4},{24,8},{28,12},{1,17},{... | collective-permute-start | bytes 319496 | tf_op jit(solution)/shard_map/ppermute | solution.py:169
  81.4 8.0 %collective-permute-start.9 = (f32[26,1024]{1,0:T(8,128)S(1)}, f32[26,1024]{1,0:T(8,128)S(1)}, u32[]{:S(2)}, u32[]{:S(2)}) collective-permute-start(f32[26,1024]{1,0:T(8,128)S(1)} %pad_maximum_fusion.9), channel_id=1, source_target_pairs={{0,16},{4,20},{8,24},{12,28},{16,0},{20,4},{24,8},{28,12},{1,17},{... | collective-permute-start | bytes 319496 | tf_op jit(solution)/shard_map/ppermute | solution.py:169
where the time goes:
time: 92.1 us; the launch traced here: 91.5 us
  Pallas kernels  33.2 us (36%)
  starting transfers between devices  19 us (21%)
  waiting for transfers between devices  15.7 us (17%)
  local copies, waits for them, and re-layouts  14.4 us (16%)
  other arithmetic  8.22 us (9%)
  between operations  0.93 us (1%)
    pallas_call x2, Pallas kernels, body(): pl.pallas_call(functools.partial(kernel, n, length, len(outs)), grid=(ste...  33.2 us
    ppermute x6, waiting for transfers between devices, reduce_parts(): got = lax.ppermute(pack, axis, [(i, i ^ dist) for i in range(size)])  15.7 us
    ppermute x4, starting transfers between devices, shifted(): return lax.ppermute(value, axis, pairs)  11.6 us
    ppermute x6, starting transfers between devices, reduce_parts(): got = lax.ppermute(pack, axis, [(i, i ^ dist) for i in range(size)])  7.37 us
    rev x1, local copies, waits for them, and re-layouts, body(): hrev = hg[::-1]  5.36 us
    unnamed x13, local copies, waits for them, and re-layouts  2.93 us
    select_n x2, other arithmetic, reduce_parts(): keep = jnp.where(bit == 0, pair[:, 0], pair[:, 1])  2.15 us
  transfers between devices with their start and end apart: 10, of which 4 were waited for; matrix products, arithmetic and copies ran while one was open for 16% of the time, Pallas kernels for 36%

commit v1 on v0

--- a/solution.py
+++ b/solution.py
@@ -37,7 +37,7 @@
     return jnp.dot(mat, jnp.concatenate([hi, lo, hi], 0), preferred_element_type=F32)
 
 
-def kernel(span, length, nalias, q_r, k_r, v_r, g_r, fwd_r, bwd_r, sf_r, h_r, hrev_r, fm_r, im_r, *rest):
+def kernel(span, length, nalias, q_r, k_r, v_r, g_r, fwd_r, bwd_r, sf_r, h_r, gain_r, fm_r, im_r, rev_r, *rest):
     rest = rest[nalias:]
     oq_r, ok_r, ov_r, pl_r, ps_r = rest[:5]
     xq, xk, xv, kf, vf, zs, gs, gq, gk, gv, zsp, gsp = rest[5:]
@@ -90,7 +90,8 @@
     qb = feat(xq, EDGE, t0, 8, sf[0])
     gs[t0 : t0 + 8] = qb * bwd_r[halo + n : halo + n + EDGE].astype(F32)[0:8]
 
-    h = h_r[...]
+    row0 = lax.broadcasted_iota(jnp.int32, (n, 1), 0) == 0
+    h = h_r[...] + jnp.where(row0, gain_r[...], 0.0)
     hsp = dot3(fm, h)
     hr, hi = hsp[0:n], hsp[n:]
     lr = li = None
@@ -115,7 +116,9 @@
     long = dot3(im, jnp.concatenate([lr, li], 0))
     pl_r[...] = long
 
-    hrev = hrev_r[...]
+    hhi = h.astype(BF16)
+    hlo = (h - hhi.astype(F32)).astype(BF16)
+    hrev = jnp.dot(rev_r[...], jnp.concatenate([hhi, hlo], 0), preferred_element_type=F32)
     g_edge = bwd_r[halo : halo + EDGE].astype(F32)
     for r in range(taps - 1):
         at = length + n - (n - 1) + r
@@ -142,6 +145,30 @@
     rows.append(long[0:1])
     for i, row in enumerate(rows):
         ps_r[i : i + 1] = row
+
+
+def pack_kernel(halo, length, cw, q_r, k_r, v_r, g_r, *rest):
+    outs, sem = rest[:-1], rest[-1]
+    copies = []
+
+    def put(src, start, rows, c, dst, at):
+        copy = pltpu.make_async_copy(
+            src.at[pl.ds(start, rows), pl.ds(c * cw, cw)], dst.at[pl.ds(at, rows)], sem.at[len(copies)]
+        )
+        copy.start()
+        copies.append(copy)
+
+    for c in range(CHUNKS):
+        tail, head = outs[2 * c], outs[2 * c + 1]
+        put(k_r, length - halo, halo, c, tail, 0)
+        put(v_r, length - halo, halo, c, tail, halo)
+        put(q_r, length - EDGE, EDGE, c, tail, 2 * halo)
+        put(q_r, 0, halo, c, head, 0)
+        put(g_r, 0, halo, c, head, halo)
+        put(k_r, 0, EDGE, c, head, 2 * halo)
+        put(v_r, 0, EDGE, c, head, 2 * halo + EDGE)
+    for copy in copies:
+        copy.wait()
 
 
 def shifted(value, axis, by):
@@ -184,16 +211,20 @@
     fm, im = matrices(n)
     fm = jnp.asarray(fm)
     im = jnp.asarray(im)
-    hg = long_filter.at[0].add(skip_gain)
-    hrev = hg[::-1]
+    flip = np.eye(n, dtype=np.float32)[::-1]
+    rev = jnp.asarray(np.concatenate([flip, flip], 1).astype(BF16))
+    gain = skip_gain.reshape(1, width)
     arrays = (input_q, input_k, input_v, grad_out)
     outs = ()
-    halos = []
-    for c in range(CHUNKS):
-        cs = slice(c * cw, (c + 1) * cw)
-        tail = jnp.concatenate([input_k[length - halo :, cs], input_v[length - halo :, cs], input_q[length - EDGE :, cs]], 0)
-        head = jnp.concatenate([input_q[:halo, cs], grad_out[:halo, cs], input_k[:EDGE, cs], input_v[:EDGE, cs]], 0)
-        halos.append((shifted(tail, "seq", 1), shifted(head, "seq", -1)))
+    packed = pl.pallas_call(
+        functools.partial(pack_kernel, halo, length, cw),
+        in_specs=[pl.BlockSpec(memory_space=pl.ANY)] * 4,
+        out_specs=[pl.BlockSpec(memory_space=pl.ANY)] * (2 * CHUNKS),
+        out_shape=[jax.ShapeDtypeStruct((2 * halo + EDGE * (1 + i % 2), cw), BF16) for i in range(2 * CHUNKS)],
+        scratch_shapes=[pltpu.SemaphoreType.DMA((7 * CHUNKS,))],
+        name="pack",
+    )(*arrays)
+    halos = [(shifted(packed[2 * c], "seq", 1), shifted(packed[2 * c + 1], "seq", -1)) for c in range(CHUNKS)]
     small_rows = 3 * taps + 1
     parts = []
     for c in range(CHUNKS):
@@ -211,9 +242,10 @@
                 pl.BlockSpec((bwd.shape[0], lanes), own),
                 pl.BlockSpec((3, taps, lanes), lambda i, c=c: (0, 0, c * steps + i)),
                 pl.BlockSpec((n, lanes), col),
-                pl.BlockSpec((n, lanes), col),
+                pl.BlockSpec((1, lanes), col),
                 fixed(fm),
                 fixed(im),
+                fixed(rev),
             ]
             + [pl.BlockSpec(memory_space=pl.ANY)] * len(outs),
             out_specs=[full] * 3 + [pl.BlockSpec((n, lanes), own), pl.BlockSpec((small_rows, lanes), own)],
@@ -233,9 +265,9 @@
                 pltpu.VMEM((length // n + 1, 2 * n, lanes), F32),
                 pltpu.VMEM((length // n + 1, 2 * n, lanes), F32),
             ],
-            input_output_aliases={11 + j: j for j in range(len(outs))},
+            input_output_aliases={12 + j: j for j in range(len(outs))},
             name=f"hyena_bwd_{c}",
-        )(*arrays, fwd, bwd, short_filters, hg, hrev, fm, im, *outs)
+        )(*arrays, fwd, bwd, short_filters, long_filter, gain, fm, im, rev, *outs)
         outs = tuple(res[:3])
         parts.append(reduce_parts(res[3], res[4], "seq"))
     grad_long = jnp.concatenate([p[0] for p in parts], 1)

time: 92.1 us -> 162 us (1.76)
  Pallas kernels: 33.2 us -> 114 us
  local copies, waits for them, and re-layouts: 14.4 us -> 2.86 us
  other arithmetic: 8.22 us -> 5.53 us
  waiting for transfers between devices: 15.7 us -> 17.7 us
  starting transfers between devices: 19 us -> 20.9 us
    pallas_call x0 -> x1, Pallas kernels: none -> 78.7 us  [body(): pl.pallas_call(functools.partial(pack_kernel, halo, length, cw), in_specs...]
    rev x1 -> x0, local copies, waits for them, and re-layouts: 5.36 us -> none  [body(): hrev = hg[::-1]]
    slice x5 -> x0, local copies, waits for them, and re-layouts: 5.13 us -> none  [the longest x1 1.34 us: body(): input_k[length - halo:, cs]]
    concatenate x4 -> x0, other arithmetic: 2.69 us -> none  [the longest x2 1.75 us: body(): jnp.concatenate([input_k[length - halo:, cs], input_v[length - halo:, cs]...]
    ppermute x6, starting transfers between devices: 7.37 us -> 10.1 us  [reduce_parts(): got = lax.ppermute(pack, axis, [(i, i ^ dist) for i in range(size)])]
    pallas_call x2, Pallas kernels: 33.2 us -> 35.4 us  [body(): pl.pallas_call(functools.partial(kernel, n, length, len(outs)), grid=(ste...]
    ppermute x6, waiting for transfers between devices: 15.7 us -> 17.7 us  [reduce_parts(): got = lax.ppermute(pack, axis, [(i, i ^ dist) for i in range(size)])]
  transfers between devices with their start and end apart: 10 -> 10, of which waited for: 4 -> 4; matrix products, arithmetic and copies ran while one was open for 16% -> 3% of each run, Pallas kernels for 36% -> 22%
where the time goes in v1:
time: 162 us
  Pallas kernels  114 us (70%)
  starting transfers between devices  20.9 us (13%)
  waiting for transfers between devices  17.7 us (11%)
  other arithmetic  5.53 us (3%)
  local copies, waits for them, and re-layouts  2.86 us (2%)
    pallas_call x1, Pallas kernels, body(): pl.pallas_call(functools.partial(pack_kernel, halo, length, cw), in_specs...  78.7 us
    pallas_call x2, Pallas kernels, body(): pl.pallas_call(functools.partial(kernel, n, length, len(outs)), grid=(ste...  35.4 us
    ppermute x6, waiting for transfers between devices, reduce_parts(): got = lax.ppermute(pack, axis, [(i, i ^ dist) for i in range(size)])  17.7 us
    ppermute x4, starting transfers between devices, shifted(): return lax.ppermute(value, axis, pairs)  10.9 us
    ppermute x6, starting transfers between devices, reduce_parts(): got = lax.ppermute(pack, axis, [(i, i ^ dist) for i in range(size)])  10.1 us
  transfers between devices with their start and end apart: 10, of which 4 were waited for; matrix products, arithmetic and copies ran while one was open for 3% of the time, Pallas kernels for 22%

profile of v1, /device:TPU:0, one launch (start us, length us, event | category | flops | bytes accessed | tf_op | source)
XLA Modules:
  0.0 162.0 jit_solution(5214322211111880666)
XLA Ops:
  0.6 78.7 %pack.1 = (bf16[304,1024]{1,0:T(8,128)(2,1)}, bf16[320,1024]{1,0:T(8,128)(2,1)}, bf16[304,1024]{1,0:T(8,128)(2,1)}, bf16[320,1024]{1,0:T(8,128)(2,1)}) custom-call(bf16[512,2048]{1,0:T(8,128)(2,1)} %q_r.5, bf16[512,2048]{1,0:T(8,128)(2,1)} %k_r.5, bf16[512,2048]{1,0:T(8,128)(2,1)} %v_r.5, bf16[512,2048]{1,0:T(8,128)(2,1)} %g_r.5), custom_call_target="tpu_custom_call" | custom-call | tf_op jit(solution)/shard_map/pack/pallas_call | solution.py:219
  79.3 1.3 collective-permute-start.3
  80.6 3.1 %collective-permute-start.2 = (bf16[304,1024]{1,0:T(8,128)(2,1)}, bf16[304,1024]{1,0:T(8,128)(2,1)S(1)}, u32[]{:S(2)}, u32[]{:S(2)}) collective-permute-start(bf16[304,1024]{1,0:T(8,128)(2,1)} %get-tuple-element.22), channel_id=1, source_target_pairs={{0,4},{4,8},{8,12},{12,16},{16,20},{20,24},{24,28},{1,5},{5,9},{9,... | collective-permute-start | bytes 1867784 | tf_op jit(solution)/shard_map/ppermute | solution.py:177
  83.7 1.3 collective-permute-start.1
  85.0 5.2 %collective-permute-start = (bf16[304,1024]{1,0:T(8,128)(2,1)}, bf16[304,1024]{1,0:T(8,128)(2,1)S(1)}, u32[]{:S(2)}, u32[]{:S(2)}) collective-permute-start(bf16[304,1024]{1,0:T(8,128)(2,1)} %get-tuple-element.20), channel_id=1, source_target_pairs={{0,4},{4,8},{8,12},{12,16},{16,20},{20,24},{24,28},{1,5},{5,9},{9,... | collective-permute-start | bytes 1867784 | tf_op jit(solution)/shard_map/ppermute | solution.py:177
  90.2 0.0 collective-permute-done.2.fwd_r
  90.2 0.0 copy-start.3
  90.2 0.0 collective-permute-done.3.bwd_r
  90.2 0.0 copy-start.1
  90.2 0.8 copy-done.3
  91.1 0.2 copy-done.1
  91.3 17.7 %hyena_bwd_0.1 = (bf16[512,2048]{1,0:T(8,128)(2,1)}, bf16[512,2048]{1,0:T(8,128)(2,1)}, bf16[512,2048]{1,0:T(8,128)(2,1)}, f32[128,1024]{1,0:T(8,128)}, f32[10,1024]{1,0:T(8,128)}) custom-call(bf16[512,2048]{1,0:T(8,128)(2,1)} %q_r.5, bf16[512,2048]{1,0:T(8,128)(2,1)} %k_r.5, bf16[512,2048]{1,0:T(8,128)(2,1)} %v_r.5, bf16[512,2048]{1,0:T(8,128)(2,1)} %g_r.5, ...), custom_call_target="tpu_custom_call" | custom-call | tf_op jit(solution)/shard_map/hyena_bwd_0/pallas_call | solution.py:236
  108.9 1.1 fusion.1
  110.0 0.9 pad_maximum_fusion
  110.9 3.6 %collective-permute-start.4 = (f32[74,1024]{1,0:T(8,128)S(1)}, f32[74,1024]{1,0:T(8,128)S(1)}, u32[]{:S(2)}, u32[]{:S(2)}) collective-permute-start(f32[74,1024]{1,0:T(8,128)S(1)} %pad_maximum_fusion), channel_id=1, source_target_pairs={{0,4},{4,0},{8,12},{12,8},{16,20},{20,16},{24,28},{28,24},{1,5},{5... | collective-permute-start | bytes 909320 | tf_op jit(solution)/shard_map/ppermute | solution.py:196
  114.5 0.0 collective-permute-done.fwd_r
  114.5 0.0 copy-start.2
  114.5 0.0 collective-permute-done.1.bwd_r
  114.5 0.0 copy-start
  114.5 0.8 copy-done.2
  115.4 0.2 copy-done
  115.6 17.7 %hyena_bwd_1.1 = (bf16[512,2048]{1,0:T(8,128)(2,1)}, bf16[512,2048]{1,0:T(8,128)(2,1)}, bf16[512,2048]{1,0:T(8,128)(2,1)}, f32[128,1024]{1,0:T(8,128)}, f32[10,1024]{1,0:T(8,128)}) custom-call(bf16[512,2048]{1,0:T(8,128)(2,1)} %q_r.5, bf16[512,2048]{1,0:T(8,128)(2,1)} %k_r.5, ...), custom_call_target="tpu_custom_call", output_to_operand_aliasing={{0}: (12, {}), {1}: (13, {}), {2}: (14, {})} | custom-call | tf_op jit(solution)/shard_map/hyena_bwd_1/pallas_call | solution.py:236
  133.3 1.1 fusion.3
  134.4 0.0 copy-start.4
  134.4 0.9 pad_maximum_fusion.1
  135.3 0.0 copy-start.5
  135.3 0.1 collective-permute-start.7
  135.5 0.0 collective-permute-done.4
  135.5 1.5 collective-permute-done.7
  137.1 0.0 copy-done.4
  137.2 2.5 %collective-permute-start.5 = (f32[42,1024]{1,0:T(8,128)S(1)}, f32[42,1024]{1,0:T(8,128)S(1)}, u32[]{:S(2)}, u32[]{:S(2)}) collective-permute-start(f32[42,1024]{1,0:T(8,128)S(1)} %pad_maximum_fusion.2), channel_id=1, source_target_pairs={{0,8},{4,12},{8,0},{12,4},{16,24},{20,28},{24,16},{28,20},{1,9},{5... | collective-permute-start | bytes 516104 | tf_op jit(solution)/shard_map/ppermute | solution.py:196
  139.6 0.0 copy-done.5
  139.7 0.1 collective-permute-start.8
  139.8 5.6 %collective-permute-done.5 = f32[42,1024]{1,0:T(8,128)S(1)} collective-permute-done((f32[42,1024]{1,0:T(8,128)S(1)}, f32[42,1024]{1,0:T(8,128)S(1)}, u32[]{:S(2)}, u32[]{:S(2)}) %collective-permute-start.5) | collective-permute-done | bytes 172064 | tf_op jit(solution)/shard_map/ppermute | solution.py:196
  145.5 3.1 %collective-permute-start.6 = (f32[26,1024]{1,0:T(8,128)S(1)}, f32[26,1024]{1,0:T(8,128)S(1)}, u32[]{:S(2)}, u32[]{:S(2)}) collective-permute-start(f32[26,1024]{1,0:T(8,128)S(1)} %pad_maximum_fusion.4), channel_id=1, source_target_pairs={{0,16},{4,20},{8,24},{12,28},{16,0},{20,4},{24,8},{28,12},{1,17},{... | collective-permute-start | bytes 319496 | tf_op jit(solution)/shard_map/ppermute | solution.py:196
  148.6 3.4 %collective-permute-done.8 = f32[42,1024]{1,0:T(8,128)S(1)} collective-permute-done((f32[42,1024]{1,0:T(8,128)S(1)}, f32[42,1024]{1,0:T(8,128)S(1)}, u32[]{:S(2)}, u32[]{:S(2)}) %collective-permute-start.8) | collective-permute-done | bytes 172064 | tf_op jit(solution)/shard_map/ppermute | solution.py:196
  152.1 0.7 collective-permute-start.9
  152.8 0.0 collective-permute-done.6
  152.8 7.1 %collective-permute-done.9 = f32[26,1024]{1,0:T(8,128)S(1)} collective-permute-done((f32[26,1024]{1,0:T(8,128)S(1)}, f32[26,1024]{1,0:T(8,128)S(1)}, u32[]{:S(2)}, u32[]{:S(2)}) %collective-permute-start.9) | collective-permute-done | bytes 106528 | tf_op jit(solution)/shard_map/ppermute | solution.py:196
  160.0 0.6 pad_maximum_fusion.7
  160.6 0.7 reshape.163
  161.3 0.7 pad_maximum_fusion.6
  (24 shorter events, 0.4 us)
Async XLA Ops:
  79.3 10.9 %collective-permute-start.3 = (bf16[320,1024]{1,0:T(8,128)(2,1)}, bf16[320,1024]{1,0:T(8,128)(2,1)S(1)}, u32[]{:S(2)}, u32[]{:S(2)}) collective-permute-start(bf16[320,1024]{1,0:T(8,128)(2,1)} %get-tuple-element.23), channel_id=1, source_target_pairs={{4,0},{8,4},{12,8},{16,12},{20,16},{24,20},{28,24},{5,1},{9,5},{13... | collective-permute-start | bytes 1966088 | tf_op jit(solution)/shard_map/ppermute | solution.py:177
  80.6 9.6 %collective-permute-start.2 = (bf16[304,1024]{1,0:T(8,128)(2,1)}, bf16[304,1024]{1,0:T(8,128)(2,1)S(1)}, u32[]{:S(2)}, u32[]{:S(2)}) collective-permute-start(bf16[304,1024]{1,0:T(8,128)(2,1)} %get-tuple-element.22), channel_id=1, source_target_pairs={{0,4},{4,8},{8,12},{12,16},{16,20},{20,24},{24,28},{1,5},{5,9},{9,... | collective-permute-start | bytes 1867784 | tf_op jit(solution)/shard_map/ppermute | solution.py:177
  83.7 30.9 %collective-permute-start.1 = (bf16[320,1024]{1,0:T(8,128)(2,1)}, bf16[320,1024]{1,0:T(8,128)(2,1)S(1)}, u32[]{:S(2)}, u32[]{:S(2)}) collective-permute-start(bf16[320,1024]{1,0:T(8,128)(2,1)} %get-tuple-element.21), channel_id=1, source_target_pairs={{4,0},{8,4},{12,8},{16,12},{20,16},{24,20},{28,24},{5,1},{9,5},{13... | collective-permute-start | bytes 1966088 | tf_op jit(solution)/shard_map/ppermute | solution.py:177
  85.0 29.5 %collective-permute-start = (bf16[304,1024]{1,0:T(8,128)(2,1)}, bf16[304,1024]{1,0:T(8,128)(2,1)S(1)}, u32[]{:S(2)}, u32[]{:S(2)}) collective-permute-start(bf16[304,1024]{1,0:T(8,128)(2,1)} %get-tuple-element.20), channel_id=1, source_target_pairs={{0,4},{4,8},{8,12},{12,16},{16,20},{20,24},{24,28},{1,5},{5,9},{9,... | collective-permute-start | bytes 1867784 | tf_op jit(solution)/shard_map/ppermute | solution.py:177
  90.2 0.8 copy-start.3
  90.2 1.0 copy-start.1
  110.9 24.6 %collective-permute-start.4 = (f32[74,1024]{1,0:T(8,128)S(1)}, f32[74,1024]{1,0:T(8,128)S(1)}, u32[]{:S(2)}, u32[]{:S(2)}) collective-permute-start(f32[74,1024]{1,0:T(8,128)S(1)} %pad_maximum_fusion), channel_id=1, source_target_pairs={{0,4},{4,0},{8,12},{12,8},{16,20},{20,16},{24,28},{28,24},{1,5},{5... | collective-permute-start | bytes 909320 | tf_op jit(solution)/shard_map/ppermute | solution.py:196
  114.5 0.8 copy-start.2
  114.5 1.1 copy-start
  134.4 2.7 %copy-start.4 = (f32[10,1024]{1,0:T(8,128)S(1)}, f32[10,1024]{1,0:T(8,128)}, u32[]{:S(2)}) copy-start(f32[10,1024]{1,0:T(8,128)} %get-tuple-element.31) | copy-start | bytes 122884
  135.3 4.3 %copy-start.5 = (f32[10,1024]{1,0:T(8,128)S(1)}, f32[10,1024]{1,0:T(8,128)}, u32[]{:S(2)}) copy-start(f32[10,1024]{1,0:T(8,128)} %get-tuple-element.33) | copy-start | bytes 122884
  135.3 1.7 %collective-permute-start.7 = (f32[74,1024]{1,0:T(8,128)S(1)}, f32[74,1024]{1,0:T(8,128)S(1)}, u32[]{:S(2)}, u32[]{:S(2)}) collective-permute-start(f32[74,1024]{1,0:T(8,128)S(1)} %pad_maximum_fusion.1), channel_id=1, source_target_pairs={{0,4},{4,0},{8,12},{12,8},{16,20},{20,16},{24,28},{28,24},{1,5},{5... | collective-permute-start | bytes 909320 | tf_op jit(solution)/shard_map/ppermute | solution.py:196
  137.2 8.2 %collective-permute-start.5 = (f32[42,1024]{1,0:T(8,128)S(1)}, f32[42,1024]{1,0:T(8,128)S(1)}, u32[]{:S(2)}, u32[]{:S(2)}) collective-permute-start(f32[42,1024]{1,0:T(8,128)S(1)} %pad_maximum_fusion.2), channel_id=1, source_target_pairs={{0,8},{4,12},{8,0},{12,4},{16,24},{20,28},{24,16},{28,20},{1,9},{5... | collective-permute-start | bytes 516104 | tf_op jit(solution)/shard_map/ppermute | solution.py:196
  139.7 12.3 %collective-permute-start.8 = (f32[42,1024]{1,0:T(8,128)S(1)}, f32[42,1024]{1,0:T(8,128)S(1)}, u32[]{:S(2)}, u32[]{:S(2)}) collective-permute-start(f32[42,1024]{1,0:T(8,128)S(1)} %pad_maximum_fusion.3), channel_id=1, source_target_pairs={{0,8},{4,12},{8,0},{12,4},{16,24},{20,28},{24,16},{28,20},{1,9},{5... | collective-permute-start | bytes 516104 | tf_op jit(solution)/shard_map/ppermute | solution.py:196
  145.5 7.3 %collective-permute-start.6 = (f32[26,1024]{1,0:T(8,128)S(1)}, f32[26,1024]{1,0:T(8,128)S(1)}, u32[]{:S(2)}, u32[]{:S(2)}) collective-permute-start(f32[26,1024]{1,0:T(8,128)S(1)} %pad_maximum_fusion.4), channel_id=1, source_target_pairs={{0,16},{4,20},{8,24},{12,28},{16,0},{20,4},{24,8},{28,12},{1,17},{... | collective-permute-start | bytes 319496 | tf_op jit(solution)/shard_map/ppermute | solution.py:196
  152.1 7.8 %collective-permute-start.9 = (f32[26,1024]{1,0:T(8,128)S(1)}, f32[26,1024]{1,0:T(8,128)S(1)}, u32[]{:S(2)}, u32[]{:S(2)}) collective-permute-start(f32[26,1024]{1,0:T(8,128)S(1)} %pad_maximum_fusion.5), channel_id=1, source_target_pairs={{0,16},{4,20},{8,24},{12,28},{16,0},{20,4},{24,8},{28,12},{1,17},{... | collective-permute-start | bytes 319496 | tf_op jit(solution)/shard_map/ppermute | solution.py:196
